TPU v7x, 8 devices: a whole 2x2x1 slice. The times are simulated.
8 devices in a mesh: dp: 1 (over z), tp: 2 (over y), ep: 4 (over x, core).
Axes of the slice: x: 2, y: 2, z: 1, core: 2. Of those that a mesh axis runs over, the one named last changes fastest.
Arguments:
- hidden: bfloat16 [256, 2048], P(('dp', 'ep'))
- seq_lens: int32 [256], P(('dp', 'ep'))
- rope_cos: float32 [256, 64], P(('dp', 'ep'))
- rope_sin: float32 [256, 64], P(('dp', 'ep'))
- ln1_scale: bfloat16 [2048], replicated
- ln1_bias: bfloat16 [2048], replicated
- w_qkv: bfloat16 [2048, 5120], P(None, 'tp')
- b_qkv: bfloat16 [5120], P('tp')
- w_out: bfloat16 [4096, 2048], P('tp')
- b_out: bfloat16 [2048], replicated
- k_cache: bfloat16 [256, 128, 4, 128], P(('dp', 'ep'), None, 'tp')
- v_cache: bfloat16 [256, 128, 4, 128], P(('dp', 'ep'), None, 'tp')
- ln2_scale: bfloat16 [2048], replicated
- ln2_bias: bfloat16 [2048], replicated
- w_router: bfloat16 [2048, 128], replicated
- expert_ids: int32 [256, 8], P(('dp', 'ep'))
- w_gate: bfloat16 [128, 2048, 768], P('ep', None, 'tp')
- w_up: bfloat16 [128, 2048, 768], P('ep', None, 'tp')
- w_down: bfloat16 [128, 768, 2048], P('ep', 'tp')
Outputs:
- output 1: bfloat16 [256, 2048], P(('dp', 'ep'))
- output 2: bfloat16 [256, 128, 4, 128], P(('dp', 'ep'), None, 'tp')
- output 3: bfloat16 [256, 128, 4, 128], P(('dp', 'ep'), None, 'tp')
All inputs are finite; a program needn't handle non-finite values.
Results may differ from a plain program's by a relative error of at most 0.0107399.
Values are sent between devices in bfloat16 or wider.
A program may use at most 1 GiB of HBM per device.

v0:
```python
import jax
import jax.numpy as jnp
from jax import lax
from jax.sharding import PartitionSpec as P

EPS = 1e-5


def layer_norm(values, ln_scale, ln_bias):
    vals_f32 = values.astype(jnp.float32)
    row_mean = jnp.mean(vals_f32, axis=-1, keepdims=True)
    centered = vals_f32 - row_mean
    row_var = jnp.mean(centered * centered, axis=-1, keepdims=True)
    normed = centered * lax.rsqrt(row_var + EPS)
    return (normed * ln_scale.astype(jnp.float32) + ln_bias.astype(jnp.float32)).astype(jnp.bfloat16)


def apply_rope(values, cos_part, sin_part):
    half_dim = values.shape[-1] // 2
    vals_f32 = values.astype(jnp.float32)
    first_half = vals_f32[..., :half_dim]
    second_half = vals_f32[..., half_dim:]
    rotated = jnp.concatenate([first_half * cos_part - second_half * sin_part, second_half * cos_part + first_half * sin_part], axis=-1)
    return rotated.astype(jnp.bfloat16)


def attention_part(normed, seq_lens, rope_cos, rope_sin, w_qkv, b_qkv, w_out, k_cache, v_cache):
    n_batch, s_max, n_groups, head_dim = k_cache.shape
    q_per = w_qkv.shape[1] // (n_groups * head_dim) - 2
    qkv_rows = (jnp.dot(normed, w_qkv, preferred_element_type=jnp.float32) + b_qkv.astype(jnp.float32)).astype(jnp.bfloat16)
    qkv_rows = qkv_rows.reshape(n_batch, n_groups, q_per + 2, head_dim)
    queries = apply_rope(qkv_rows[:, :, :q_per], rope_cos[:, None, None, :], rope_sin[:, None, None, :])
    key_new = apply_rope(qkv_rows[:, :, q_per], rope_cos[:, None, :], rope_sin[:, None, :])
    value_new = qkv_rows[:, :, q_per + 1]
    positions = jnp.arange(s_max)
    write_mask = (positions[None, :] == seq_lens[:, None])[:, :, None, None]
    k_cache_out = jnp.where(write_mask, key_new[:, None], k_cache)
    v_cache_out = jnp.where(write_mask, value_new[:, None], v_cache)
    scores = jnp.einsum('bgqh,bsgh->bgqs', queries, k_cache_out, preferred_element_type=jnp.float32) * head_dim ** -0.5
    in_range = positions[None, None, None, :] <= seq_lens[:, None, None, None]
    attn_probs = jax.nn.softmax(jnp.where(in_range, scores, -jnp.inf), axis=-1).astype(jnp.bfloat16)
    context = jnp.einsum('bgqs,bsgh->bgqh', attn_probs, v_cache_out, preferred_element_type=jnp.float32).astype(jnp.bfloat16)
    attn_part = jnp.dot(context.reshape(n_batch, n_groups * q_per * head_dim), w_out, preferred_element_type=jnp.float32)
    return attn_part, k_cache_out, v_cache_out


def route_tables(expert_ids, gate_probs, first_expert, n_exp, capacity):
    id_match = expert_ids[..., None] == (first_expert + jnp.arange(n_exp))
    chosen_mask = jnp.sum(id_match.astype(jnp.int32), axis=-2)
    slot_rank = jnp.cumsum(chosen_mask, axis=-2) - chosen_mask
    slot_of = jnp.swapaxes(jnp.where(chosen_mask > 0, slot_rank, -1), -1, -2)
    dispatch = (slot_of[..., None, :] == jnp.arange(capacity)[:, None]).astype(jnp.bfloat16)
    gate_dense = jnp.sum(jnp.where(id_match, gate_probs[..., None].astype(jnp.float32), 0.0), axis=-2)
    combine = dispatch * jnp.swapaxes(gate_dense, -1, -2)[..., None, :].astype(jnp.bfloat16)
    return dispatch, combine


def expert_ffn(routed_rows, w_gate, w_up, w_down):
    gate_pre = jnp.einsum('secd,edf->escf', routed_rows, w_gate, preferred_element_type=jnp.float32)
    up_pre = jnp.einsum('secd,edf->escf', routed_rows, w_up, preferred_element_type=jnp.float32)
    hidden_act = (jax.nn.silu(gate_pre) * up_pre).astype(jnp.bfloat16)
    return jnp.einsum('escf,efd->escd', hidden_act, w_down, preferred_element_type=jnp.float32)


def solution(mesh):
    n_ep = mesh.shape['ep']
    token_rows = P(('dp', 'ep'), None)
    token_vec = P(('dp', 'ep'))
    cache_spec = P(('dp', 'ep'), None, 'tp', None)
    expert_in = P('ep', None, 'tp')
    expert_down = P('ep', 'tp', None)

    def device_step(hidden, seq_lens, rope_cos, rope_sin, ln1_scale, ln1_bias, w_qkv, b_qkv, w_out, b_out, k_cache, v_cache, ln2_scale, ln2_bias, w_router, expert_ids, w_gate, w_up, w_down):
        n_batch, d_model = hidden.shape
        e_local = w_gate.shape[0]
        n_exp = e_local * n_ep
        top_k = expert_ids.shape[1]
        capacity = (2 * top_k * n_batch + n_exp - 1) // n_exp
        normed = layer_norm(hidden, ln1_scale, ln1_bias)
        attn_part, k_cache_out, v_cache_out = attention_part(normed, seq_lens, rope_cos, rope_sin, w_qkv, b_qkv, w_out, k_cache, v_cache)
        attn_sum = lax.psum(attn_part.astype(jnp.bfloat16), 'tp')
        hidden_mid = (hidden.astype(jnp.float32) + attn_sum.astype(jnp.float32) + b_out.astype(jnp.float32)).astype(jnp.bfloat16)
        normed2 = layer_norm(hidden_mid, ln2_scale, ln2_bias)
        logits = jnp.dot(normed2, w_router, preferred_element_type=jnp.float32)
        gate_probs = jax.nn.softmax(jnp.take_along_axis(logits, expert_ids, axis=1), axis=-1).astype(jnp.bfloat16)
        dispatch, combine = route_tables(expert_ids, gate_probs, 0, n_exp, capacity)
        outgoing = jnp.einsum('ecb,bd->ecd', dispatch, normed2, preferred_element_type=jnp.float32).astype(jnp.bfloat16)
        received = lax.all_to_all(outgoing, 'ep', 0, 0, tiled=True).reshape(n_ep, e_local, capacity, d_model)
        down_part = expert_ffn(received, w_gate, w_up, w_down).astype(jnp.bfloat16)
        expert_out = lax.psum(down_part, 'tp')
        returned = lax.all_to_all(expert_out, 'ep', 1, 0, tiled=True).reshape(n_exp, capacity, d_model)
        moe_sum = jnp.einsum('ecb,ecd->bd', combine, returned, preferred_element_type=jnp.float32)
        hidden_out = (hidden_mid.astype(jnp.float32) + moe_sum).astype(jnp.bfloat16)
        return hidden_out, k_cache_out, v_cache_out

    in_specs = (token_rows, token_vec, token_rows, token_rows, P(), P(), P(None, 'tp'), P('tp'), P('tp', None), P(), cache_spec, cache_spec, P(), P(), P(), token_rows, expert_in, expert_in, expert_down)
    return jax.shard_map(device_step, mesh=mesh, in_specs=in_specs, out_specs=(token_rows, cache_spec, cache_spec), check_vma=False)
```

profile of v0, /device:TPU:0, one launch (start us, length us, event | category | flops | bytes accessed | tf_op | source)
XLA Modules:
  0.0 355.7 jit_solution(7063784532139693804)
XLA Ops:
  7.2 1.1 convert_reduce_fusion.1
  8.4 1.2 fusion.56
  9.6 0.7 convert_element_type.100
  10.3 0.7 convert_element_type.101
  11.0 0.7 convert_element_type.103
  11.7 6.1 %fusion.18 = bf16[64,2560]{1,0:T(8,128)(2,1)S(1)} fusion(bf16[2048,2560]{1,0:T(8,128)(2,1)} %param.25, f32[2560]{0:T(1024)S(1)} %convert_element_type.103, bf16[64,2048]{1,0:T(8,128)(2,1)} %param.19, f32[2048]{0:T(1024)S(1)} %convert_element_type.101, f32[2048]{0:T(1024)S(1)} %convert_element_type.100, f32[64]{0:T(128)S(1)} %add_rsqrt_fusion.1, ...), kind=kOutput, calls=%fused_computation.21 | convolution fusion | flops 672202752 | bytes 11102720 | tf_op jit(solution)/shard_map/dot_general | solution.py:30
  18.8 13.8 %broadcast_select_fusion.1 = (bf16[64,128,2,128]{3,2,1,0:T(2,128)(2,1)}, bf16[64,128,2,128]{3,2,1,0:T(2,128)(2,1)}) fusion(bf16[64,128,2,128]{3,2,1,0:T(2,128)(2,1)} %param.29, pred[64,128]{1,0:T(8,128)(4,1)S(1)} %get-tuple-element.14, bf16[64,2,128]{2,1,0:T(2,128)(2,1)S(1)} %pad_maximum_fusion, bf16[64,128,2,128]{3,2,1,0:T(2,128)(2,1)} %param.30, ...), kind=kLoop, calls=%fused_computation.9 | loop fusion | flops 4194304 | bytes 16850944 | tf_op jit(solution)/shard_map/jit(_where)/select_n | solution.py:37
  32.6 4.7 %fusion.90 = (f32[64,2,8]{2,1,0:T(2,128)S(1)}, f32[64,2,8,128]{3,2,1,0:T(8,128)S(1)}) fusion(bf16[64,128,2,128]{3,2,1,0:T(2,128)(2,1)} %get-tuple-element.11, bf16[64,2,8,64]{3,2,1,0:T(8,128)(2,1)S(1)} %get-tuple-element.6, bf16[64,2,8,64]{3,2,1,0:T(8,128)(2,1)S(1)} %get-tuple-element.5, pred[64,128]{1,0:T(8,128)(4,1)S(1)} %get-tuple-element.13), kind=kOutput, calls=%fused_computation.101 | convolution fusion | flops 34603136 | bytes 4993024 | tf_op jit(solution)/shard_map/sub | solution.py:41
  37.3 3.4 fusion.44
  40.8 5.7 %convolution_convert_fusion.1 = bf16[64,2048]{1,0:T(8,128)(2,1)} fusion(bf16[2048,2048]{1,0:T(8,128)(2,1)} %param.27, bf16[8,8,16,128]{3,2,1,0:T(8,128)(2,1)S(1)} %bitcast.64), kind=kOutput, calls=%fused_computation.24 | convolution fusion | flops 537001984 | bytes 8912896 | tf_op jit(solution)/shard_map/dot_general | solution.py:43
  47.0 20.0 %all-reduce.3.cloned.1.call-done = bf16[64,2048]{1,0:T(8,128)(2,1)} async-done(((bf16[64,2048]{1,0:T(8,128)(2,1)}), bf16[64,2048]{1,0:T(8,128)(2,1)}) %all-reduce.3.cloned.1.call-update) | async-done | bytes 262160 | tf_op jit(solution)/shard_map/psum | solution.py:81
  67.0 1.1 convert_reduce_fusion
  68.4 1.3 convolution_convert_fusion
  69.8 2.3 copy.91
  72.1 51.5 %all_to_all.20 = bf16[128,8,2048]{2,1,0:T(8,128)(2,1)} all-to-all(bf16[128,8,2048]{2,1,0:T(8,128)(2,1)S(1)} %copy.91), channel_id=1, replica_groups=mesh['dp'=1,'tp'=2,'ep'=4] {'ep'}, dimensions={0} | all-to-all | bytes 8388608 | tf_op jit(solution)/shard_map/all_to_all | solution.py:88
  123.5 19.3 %fusion.3 = f32[32,4,8,384]{3,2,1,0:T(8,128)S(1)} fusion(bf16[32,2048,384]{2,1,0:T(8,128)(2,1)} %param.36, bf16[4,32,8,2048]{3,2,1,0:T(8,128)(2,1)} %bitcast.62), kind=kOutput, calls=%fused_computation.4 | convolution fusion | flops 1610612736 | bytes 56098816 | tf_op jit(solution)/shard_map/secd,edf->escf/dot_general | solution.py:60
  142.8 19.3 %multiply_convert_fusion.clone.4 = bf16[32,4,8,384]{3,2,1,0:T(8,128)(2,1)S(1)} fusion(f32[32,4,8,384]{3,2,1,0:T(8,128)S(1)} %fusion.3, bf16[32,2048,384]{2,1,0:T(8,128)(2,1)} %param.35, bf16[4,32,8,2048]{3,2,1,0:T(8,128)(2,1)} %bitcast.63), kind=kOutput, calls=%fused_computation.26.clone.clone.clone.1 | convolution fusion | flops 1612972032 | bytes 56885248 | tf_op jit(solution)/shard_map/secd,edf->escf/dot_general | solution.py:59
  162.1 20.5 %fusion.13 = bf16[32,4,8,2048]{3,2,1,0:T(8,128)(2,1)} fusion(bf16[32,384,2048]{2,1,0:T(8,128)(2,1)} %param.37, bf16[32,4,8,384]{3,2,1,0:T(8,128)(2,1)S(1)} %multiply_convert_fusion.clone.4), kind=kOutput, calls=%fused_computation.16 | convolution fusion | flops 1612709888 | bytes 55312384 | tf_op jit(solution)/shard_map/escf,efd->escd/dot_general | solution.py:62
  182.6 101.2 %all-reduce.5.cloned.1.call-done = bf16[32,4,8,2048]{3,2,1,0:T(8,128)(2,1)} async-done(((bf16[32,4,8,2048]{3,2,1,0:T(8,128)(2,1)}), bf16[32,4,8,2048]{3,2,1,0:T(8,128)(2,1)}) %all-reduce.5.cloned.1.call-update) | async-done | bytes 4194320 | tf_op jit(solution)/shard_map/psum | solution.py:90
  283.8 4.7 %copy.94 = bf16[32,4,8,2048]{3,2,0,1:T(8,128)(2,1)} copy(bf16[32,4,8,2048]{3,2,1,0:T(8,128)(2,1)} %all-reduce.5.cloned.1.call-done) | data formatting | bytes 8388608 | tf_op jit(solution)/shard_map/psum | solution.py:90
  288.5 5.1 %all-to-all-start.1 = ((bf16[32,4,8,2048]{3,2,0,1:T(8,128)(2,1)}), bf16[32,4,8,2048]{3,2,0,1:T(8,128)(2,1)}, u32[]{:S(2)}, u32[]{:S(2)}) async-start(bf16[32,4,8,2048]{3,2,0,1:T(8,128)(2,1)} %copy.94), calls=%async_computation.1 | async-start | bytes 8388608 | tf_op jit(solution)/shard_map/all_to_all | solution.py:91
  294.1 3.6 %gather_fusion = f32[512]{0:T(512)S(1)} fusion(f32[64,128]{1,0:T(8,128)S(1)} %fusion.87, s32[512]{0:T(512)S(1)} %reshape.157), kind=kCustom, calls=%fused_computation | custom fusion | bytes 8192 | tf_op jit(solution)/shard_map/jit(take_along_axis)/gather | solution.py:85
  298.3 43.0 %all-to-all-done.1 = bf16[32,4,8,2048]{3,2,0,1:T(8,128)(2,1)} async-done(((bf16[32,4,8,2048]{3,2,0,1:T(8,128)(2,1)}), bf16[32,4,8,2048]{3,2,0,1:T(8,128)(2,1)}, u32[]{:S(2)}, u32[]{:S(2)}) %all-to-all-start.1) | async-done | bytes 4194336 | tf_op jit(solution)/shard_map/all_to_all | solution.py:91
  341.3 7.5 %fusion.25 = bf16[64,2048]{1,0:T(8,128)(2,1)} fusion(bf16[128,8,2048]{2,1,0:T(8,128)(2,1)} %bitcast.15, bf16[64,2048]{1,0:T(8,128)(2,1)S(1)} %get-tuple-element.4, s32[128,64]{0,1:T(8,128)S(1)} %select_bitcast_fusion, bf16[128,64]{0,1:T(8,128)(2,1)S(1)} %bitcast.67), kind=kOutput, calls=%fused_computation.25 | convolution fusion | flops 268959744 | bytes 4767744 | tf_op jit(solution)/shard_map/ecb,ecd->bd/dot_general | solution.py:92
  (54 shorter events, 2.7 us)
Async XLA Ops:
  7.2 286.7 %copy-start = (bf16[2048,128]{1,0:T(8,128)(2,1)S(1)}, bf16[2048,128]{1,0:T(8,128)(2,1)}, u32[]{:S(2)}) copy-start(bf16[2048,128]{1,0:T(8,128)(2,1)} %param.33) | copy-start | bytes 1572868
  7.2 59.8 %all-reduce.3.cloned.1.call-start = ((), (), s32[]{:S(2)}) async-start(), calls=%async_computation.2 | async-start | bytes 524288 | tf_op jit(solution)/shard_map/psum | solution.py:81
  11.7 6.5 %copy-start.8 = (s32[64]{0:T(128)S(1)}, s32[64]{0:T(128)}, u32[]{:S(2)}) copy-start(s32[64]{0:T(128)} %param.20) | copy-start | bytes 772
  11.7 6.5 %copy-start.2 = (f32[64,64]{1,0:T(8,128)S(1)}, f32[64,64]{1,0:T(8,128)}, u32[]{:S(2)}) copy-start(f32[64,64]{1,0:T(8,128)} %param.22) | copy-start | bytes 49156
  11.7 6.6 %copy-start.3 = (f32[64,64]{1,0:T(8,128)S(1)}, f32[64,64]{1,0:T(8,128)}, u32[]{:S(2)}) copy-start(f32[64,64]{1,0:T(8,128)} %param.21) | copy-start | bytes 49156
  40.7 5.8 %copy-start.4 = (s32[64,8]{0,1:T(8,128)S(1)}, s32[64,8]{0,1:T(8,128)}, u32[]{:S(2)}) copy-start(s32[64,8]{0,1:T(8,128)} %param.34) | copy-start | bytes 6148
  40.8 6.1 %copy-start.5 = (bf16[2048]{0:T(1024)(128)(2,1)S(1)}, bf16[2048]{0:T(1024)(128)(2,1)}, u32[]{:S(2)}) copy-start(bf16[2048]{0:T(1024)(128)(2,1)} %param.31) | copy-start | bytes 12292
  40.8 6.1 %copy-start.6 = (bf16[2048]{0:T(1024)(128)(2,1)S(1)}, bf16[2048]{0:T(1024)(128)(2,1)}, u32[]{:S(2)}) copy-start(bf16[2048]{0:T(1024)(128)(2,1)} %param.32) | copy-start | bytes 12292
  40.8 6.1 %copy-start.7 = (bf16[2048]{0:T(1024)(128)(2,1)S(1)}, bf16[2048]{0:T(1024)(128)(2,1)}, u32[]{:S(2)}) copy-start(bf16[2048]{0:T(1024)(128)(2,1)} %param.28) | copy-start | bytes 12292
  40.8 26.2 %copy-start.1 = (bf16[64,2048]{1,0:T(8,128)(2,1)S(1)}, bf16[64,2048]{1,0:T(8,128)(2,1)}, u32[]{:S(2)}) copy-start(bf16[64,2048]{1,0:T(8,128)(2,1)} %param.19) | copy-start | bytes 786436
  46.5 237.3 %all-reduce.5.cloned.1.call-start = ((), (), s32[]{:S(2)}) async-start(), calls=%async_computation.3 | async-start | bytes 8388608 | tf_op jit(solution)/shard_map/psum | solution.py:90
  288.5 52.7 %all-to-all-start.1 = ((bf16[32,4,8,2048]{3,2,0,1:T(8,128)(2,1)}), bf16[32,4,8,2048]{3,2,0,1:T(8,128)(2,1)}, u32[]{:S(2)}, u32[]{:S(2)}) async-start(bf16[32,4,8,2048]{3,2,0,1:T(8,128)(2,1)} %copy.94), calls=%async_computation.1 | async-start | bytes 8388608 | tf_op jit(solution)/shard_map/all_to_all | solution.py:91
Sparse Core Ops, SparseCore 0:
  46.6 20.3 all-reduce.2
  182.8 100.9 all-reduce.4
where the time goes:
time: 356 us
  waiting for transfers between devices  164 us (46%)
  matrix products  88.2 us (25%)
  blocking collectives  51.5 us (14%)
  other arithmetic  20.9 us (6%)
  between operations  14.4 us (4%)
  local copies, waits for them, and re-layouts  11.5 us (3%)
  starting transfers between devices  5.16 us (1%)
    psum x1, waiting for transfers between devices, device_step(): expert_out = lax.psum(down_part, 'tp')  101 us
    all_to_all x1, blocking collectives, device_step(): lax.all_to_all(outgoing, 'ep', 0, 0, tiled=True)  51.5 us
    all_to_all x1, waiting for transfers between devices, device_step(): lax.all_to_all(expert_out, 'ep', 1, 0, tiled=True)  43 us
    dot_general x1, matrix products, expert_ffn(): jnp.einsum('escf,efd->escd', hidden_act, w_down, preferred_element_type=j...  20.5 us
    psum x1, waiting for transfers between devices, device_step(): attn_sum = lax.psum(attn_part.astype(jnp.bfloat16), 'tp')  20 us
    dot_general x1, matrix products, expert_ffn(): jnp.einsum('secd,edf->escf', routed_rows, w_gate, preferred_element_type=...  19.3 us
    dot_general x1, matrix products, expert_ffn(): jnp.einsum('secd,edf->escf', routed_rows, w_up, preferred_element_type=jn...  19.3 us
    select_n x1, other arithmetic, attention_part(): k_cache_out = jnp.where(write_mask, key_new[:, None], k_cache)  13.8 us
  transfers between devices with their start and end apart: 3, of which 3 were waited for; matrix products, arithmetic and copies ran while one was open for 1% of the time, Pallas kernels for 0%

commit v1 on v0

v1 whole, which is shorter than its diff:
```python
import functools

import jax
import jax.numpy as jnp
from jax import lax
from jax.experimental import pallas as pl
from jax.experimental.pallas import tpu as pltpu
from jax.sharding import PartitionSpec as P

EPS = 1e-5
F32 = jnp.float32
BF16 = jnp.bfloat16
MESH = pl.DeviceIdType.MESH
NT = (((1,), (1,)), ((), ()))


def layer_norm(vals_f32, scale, bias):
    row_mean = jnp.mean(vals_f32, axis=-1, keepdims=True)
    centered = vals_f32 - row_mean
    row_var = jnp.mean(centered * centered, axis=-1, keepdims=True)
    normed = centered * lax.rsqrt(row_var + EPS)
    return (normed * scale.astype(F32) + bias.astype(F32)).astype(BF16)


def attn_kernel(seq_ref, hid_ref, cos_ref, sin_ref, lns_ref, lnb_ref, bq_ref, wq_hbm, kc_hbm, vc_hbm, wo_hbm,
                part_ref, ko_hbm, vo_hbm,
                wq_buf, kbuf, vbuf, wo_buf, hbuf, qs, ks, vs, ctx, cb,
                wq_sem, k_sem, v_sem, wo_sem, ko_sem, vo_sem):
    n_b = hid_ref.shape[0]
    n_wq, _, wq_cols = wq_buf.shape
    n_wo, _, wo_cols = wo_buf.shape
    rows = kbuf.shape[1]
    heads = qs.shape[0] // n_b
    chunk = 8
    n_chunk = n_b // chunk

    def wq_copy(n):
        return pltpu.make_async_copy(wq_hbm.at[:, pl.ds(n * wq_cols, wq_cols)], wq_buf.at[n], wq_sem.at[n])

    def k_copy(c):
        return pltpu.make_async_copy(kc_hbm.at[pl.ds(c * chunk, chunk)], kbuf.at[pl.ds(c * chunk, chunk)], k_sem.at[c])

    def v_copy(c):
        return pltpu.make_async_copy(vc_hbm.at[pl.ds(c * chunk, chunk)], vbuf.at[pl.ds(c * chunk, chunk)], v_sem.at[c])

    def wo_copy(n):
        return pltpu.make_async_copy(wo_hbm.at[:, pl.ds(n * wo_cols, wo_cols)], wo_buf.at[n], wo_sem.at[n])

    def ko_copy(c):
        return pltpu.make_async_copy(kbuf.at[pl.ds(c * chunk, chunk)], ko_hbm.at[pl.ds(c * chunk, chunk)], ko_sem.at[c])

    def vo_copy(c):
        return pltpu.make_async_copy(vbuf.at[pl.ds(c * chunk, chunk)], vo_hbm.at[pl.ds(c * chunk, chunk)], vo_sem.at[c])

    for n in range(n_wq):
        wq_copy(n).start()
    for c in range(n_chunk):
        k_copy(c).start()
        v_copy(c).start()
    for n in range(n_wo):
        wo_copy(n).start()

    hbuf[...] = layer_norm(hid_ref[...].astype(F32), lns_ref[...], lnb_ref[...])
    cos2 = jnp.concatenate([cos_ref[...], cos_ref[...]], axis=1)
    sin2 = jnp.concatenate([-sin_ref[...], sin_ref[...]], axis=1)
    per_group = heads // 2 + 2
    for n in range(n_wq):
        wq_copy(n).wait()
        cols = pl.ds(n * wq_cols, wq_cols)
        qkv = jnp.dot(hbuf[...], wq_buf[n], preferred_element_type=F32) + bq_ref[:, cols].astype(F32)
        qkv = qkv.astype(BF16).astype(F32)
        for i in range(wq_cols // 128):
            g, j = divmod(n * (wq_cols // 128) + i, per_group)
            block = qkv[:, i * 128:(i + 1) * 128]
            if j <= heads // 2:
                block = block * cos2 + pltpu.roll(block, 64, 1) * sin2
                block = block.astype(BF16).astype(F32)
            if j < heads // 2:
                qs[pl.ds(g * (heads // 2) + j, n_b, stride=heads), :] = block
            elif j == heads // 2:
                ks[pl.ds(g, n_b, stride=2), :] = block
            else:
                vs[pl.ds(g, n_b, stride=2), :] = block

    col = lax.broadcasted_iota(jnp.int32, (heads, rows), 1)
    head_row = lax.broadcasted_iota(jnp.int32, (heads, rows), 0)
    own_group = (col % 2) == (head_row // (heads // 2))
    position = jnp.where(own_group, col // 2, rows)
    tile_row = lax.broadcasted_iota(jnp.int32, (16, 128), 0)
    scale = 128 ** -0.5

    def one_chunk(c, _):
        k_copy(c).wait()
        v_copy(c).wait()
        lens = [seq_ref[c * chunk + i] for i in range(chunk)]
        for i in range(chunk):
            b = c * chunk + i
            base = pl.multiple_of((lens[i] // 8) * 16, 16)
            first = lens[i] * 2 - base
            for buf, new in ((kbuf, ks), (vbuf, vs)):
                tile = buf[b, pl.ds(base, 16), :].astype(F32)
                tile = jnp.where(tile_row == first, new[pl.ds(b * 2, 1), :], tile)
                tile = jnp.where(tile_row == first + 1, new[pl.ds(b * 2 + 1, 1), :], tile)
                buf[b, pl.ds(base, 16), :] = tile.astype(BF16)
        ko_copy(c).start()
        vo_copy(c).start()
        scores = []
        for i in range(chunk):
            b = c * chunk + i
            q = qs[pl.ds(pl.multiple_of(b * heads, heads), heads), :].astype(BF16)
            s = lax.dot_general(q, kbuf[b], NT, preferred_element_type=F32) * scale
            scores.append(jnp.where(position <= lens[i], s, -jnp.inf))
        probs = []
        for i in range(chunk):
            top = jnp.max(scores[i], axis=-1, keepdims=True)
            e = jnp.exp(scores[i] - top)
            probs.append((e / jnp.sum(e, axis=-1, keepdims=True)).astype(BF16))
        for i in range(chunk):
            b = c * chunk + i
            out = jnp.dot(probs[i], vbuf[b], preferred_element_type=F32)
            ctx[pl.ds(pl.multiple_of(b * heads, heads), heads), :] = out.astype(BF16).astype(F32)
        return 0

    lax.fori_loop(0, n_chunk, one_chunk, 0)
    for j in range(heads):
        cb[:, j * 128:(j + 1) * 128] = ctx[pl.ds(j, n_b, stride=heads), :].astype(BF16)
    for n in range(n_wo):
        wo_copy(n).wait()
        part_ref[:, pl.ds(n * wo_cols, wo_cols)] = jnp.dot(cb[...], wo_buf[n], preferred_element_type=F32).astype(BF16)
    for c in range(n_chunk):
        ko_copy(c).wait()
        vo_copy(c).wait()


def attention_call(hidden, seq_lens, rope_cos, rope_sin, ln_scale, ln_bias, w_qkv, b_qkv, w_out, k_rows, v_rows):
    n_b, d_model = hidden.shape
    heads = w_out.shape[0] // 128
    vmem = pl.BlockSpec(memory_space=pltpu.VMEM)
    hbm = pl.BlockSpec(memory_space=pl.ANY)
    wq_cols = 512
    wo_cols = 512
    n_wq = w_qkv.shape[1] // wq_cols
    n_wo = d_model // wo_cols
    dma = pltpu.SemaphoreType.DMA
    return pl.pallas_call(
        attn_kernel,
        out_shape=(
            jax.ShapeDtypeStruct((n_b, d_model), BF16),
            jax.ShapeDtypeStruct(k_rows.shape, BF16),
            jax.ShapeDtypeStruct(v_rows.shape, BF16),
        ),
        in_specs=[pl.BlockSpec(memory_space=pltpu.SMEM)] + [vmem] * 6 + [hbm] * 4,
        out_specs=(vmem, hbm, hbm),
        scratch_shapes=[
            pltpu.VMEM((n_wq, d_model, wq_cols), BF16),
            pltpu.VMEM(k_rows.shape, BF16),
            pltpu.VMEM(v_rows.shape, BF16),
            pltpu.VMEM((n_wo, w_out.shape[0], wo_cols), BF16),
            pltpu.VMEM((n_b, d_model), BF16),
            pltpu.VMEM((n_b * heads, 128), F32),
            pltpu.VMEM((n_b * 2, 128), F32),
            pltpu.VMEM((n_b * 2, 128), F32),
            pltpu.VMEM((n_b * heads, 128), F32),
            pltpu.VMEM((n_b, heads * 128), BF16),
            dma((n_wq,)), dma((n_b // 8,)), dma((n_b // 8,)), dma((n_wo,)), dma((n_b // 8,)), dma((n_b // 8,)),
        ],
        compiler_params=pltpu.CompilerParams(vmem_limit_bytes=60 * 1024 * 1024),
        name="attn",
    )(seq_lens, hidden, rope_cos, rope_sin, ln_scale, ln_bias, b_qkv, w_qkv, k_rows, v_rows, w_out)


def moe_kernel(n_tp, n_ep, part_ref, hid_ref, bout_ref, lns_ref, lnb_ref, wr_ref, ids_ref, wg_hbm, wu_hbm, wd_hbm,
               out_ref,
               gbuf, ubuf, dbuf, hall, arx, x1buf, dmat, cmat, xbuf, abuf, ybuf, pbuf, rbuf, obuf,
               gsem, usem, dsem, a_send, a_recv, h_send, h_recv, r_send, r_recv, o_send, o_recv):
    me_t = lax.axis_index("tp")
    me_e = lax.axis_index("ep")
    n_dev = n_tp * n_ep
    me = me_e * n_tp + me_t
    n_gu, d_model, width = gbuf.shape
    n_dr, d_group, _, d_cols = dbuf.shape
    n_local = wg_hbm.shape[0]
    n_exp = n_local * n_ep
    half = x1buf.shape[0]
    shard = half * n_tp
    n_rows = hall.shape[0]
    cap = 32
    n_col = d_model // d_cols
    n_grp = n_local // d_group
    n_down = n_col * n_grp

    def peer_of(d):
        pid = lax.rem(me + d, n_dev)
        return pid, {"tp": lax.rem(pid, n_tp), "ep": lax.div(pid, n_tp)}

    def g_copy(i):
        slot = lax.rem(i, n_gu)
        return pltpu.make_async_copy(wg_hbm.at[i], gbuf.at[slot], gsem.at[slot])

    def u_copy(i):
        slot = lax.rem(i, n_gu)
        return pltpu.make_async_copy(wu_hbm.at[i], ubuf.at[slot], usem.at[slot])

    def d_copy(q):
        slot = lax.rem(q, n_dr)
        grp = lax.rem(q, n_grp)
        col = lax.div(q, n_grp)
        src = wd_hbm.at[pl.ds(grp * d_group, d_group), :, pl.ds(pl.multiple_of(col * d_cols, d_cols), d_cols)]
        return pltpu.make_async_copy(src, dbuf.at[slot], dsem.at[slot])

    def first_gu(i, _):
        g_copy(i).start()
        u_copy(i).start()
        return 0

    def first_d(q, _):
        d_copy(q).start()
        return 0

    lax.fori_loop(0, n_gu, first_gu, 0)
    lax.fori_loop(0, n_dr, first_d, 0)

    barrier = pltpu.get_barrier_semaphore()
    for d in range(1, n_dev):
        _, dev = peer_of(d)
        pl.semaphore_signal(barrier, inc=1, device_id=dev, device_id_type=MESH)
    pl.semaphore_wait(barrier, n_dev - 1)

    other_t = 1 - me_t
    a_copy = pltpu.make_async_remote_copy(
        src_ref=part_ref.at[pl.ds(pl.multiple_of(other_t * half, half), half)], dst_ref=arx,
        send_sem=a_send, recv_sem=a_recv, device_id={"tp": other_t, "ep": me_e}, device_id_type=MESH)
    a_copy.start()

    picked_t = jnp.zeros((n_exp, shard), F32)
    exp_row = lax.broadcasted_iota(jnp.int32, (n_exp, shard), 0)
    for k in range(ids_ref.shape[0]):
        picked_t = picked_t + (exp_row == ids_ref[pl.ds(k, 1), :]).astype(F32)
    sel = (lax.broadcasted_iota(jnp.int32, (half, shard), 1)
           == lax.broadcasted_iota(jnp.int32, (half, shard), 0) + me_t * half).astype(BF16)
    picked = lax.dot_general(sel, picked_t.astype(BF16), NT, preferred_element_type=F32)

    mine = pl.ds(pl.multiple_of(me_t * half, half), half)
    a_copy.wait()
    attn = part_ref[mine, :].astype(F32) + arx[...].astype(F32)
    x1 = (hid_ref[mine, :].astype(F32) + attn + bout_ref[...].astype(F32)).astype(BF16)
    x1buf[...] = x1
    h2 = layer_norm(x1.astype(F32), lns_ref[...], lnb_ref[...])
    my_rows = pl.ds(pl.multiple_of(me * half, half), half)
    hall[my_rows, pl.ds(0, d_model)] = h2
    logits = jnp.dot(h2, wr_ref[...], preferred_element_type=F32)
    logits = jnp.where(picked > 0.5, logits, -jnp.inf)
    e = jnp.exp(logits - jnp.max(logits, axis=-1, keepdims=True))
    gates = e / jnp.sum(e, axis=-1, keepdims=True)
    hall[my_rows, pl.ds(d_model, n_exp)] = gates.astype(BF16)

    def h_copy(d, block, dev):
        rows = pl.ds(pl.multiple_of(block * half, half), half)
        return pltpu.make_async_remote_copy(
            src_ref=hall.at[rows], dst_ref=hall.at[rows], send_sem=h_send.at[d], recv_sem=h_recv.at[block],
            device_id=dev, device_id_type=MESH)

    for d in range(1, n_dev):
        _, dev = peer_of(d)
        h_copy(d, me, dev).start()
    for d in range(1, n_dev):
        pid, dev = peer_of(d)
        h_copy(d, pid, dev).wait_recv()

    gate_cols = pl.ds(d_model, n_exp)
    pick = (lax.broadcasted_iota(jnp.int32, (n_local, n_exp), 1)
            == lax.broadcasted_iota(jnp.int32, (n_local, n_exp), 0) + me_e * n_local).astype(BF16)
    row_i = lax.broadcasted_iota(jnp.int32, (n_rows, n_rows), 0)
    col_i = lax.broadcasted_iota(jnp.int32, (n_rows, n_rows), 1)
    same = (row_i // shard) == (col_i // shard)

    gate_t = lax.dot_general(pick, hall[:, gate_cols], NT, preferred_element_type=F32)
    upper = jnp.where((row_i < col_i) & same, 1.0, 0.0).astype(BF16)
    rank_t = jnp.dot(jnp.where(gate_t > 0, 1.0, 0.0).astype(BF16), upper, preferred_element_type=F32)
    shard_t = (lax.broadcasted_iota(jnp.int32, (n_local, n_rows), 1) // shard * (cap // n_ep)).astype(F32)
    key_t = jnp.where(gate_t > 0, rank_t + shard_t, -1.0)
    slot_i = lax.broadcasted_iota(jnp.int32, (cap, n_rows), 0).astype(F32)
    for i in range(n_local):
        dmat[i * cap:(i + 1) * cap, :] = jnp.where(key_t[i:i + 1, :] == slot_i, 1.0, 0.0).astype(BF16)

    def expert_group(g, _):
        rows = pl.ds(pl.multiple_of(g * d_group * cap, d_group * cap), d_group * cap)
        for c in range(4):
            cols = pl.ds(c * (d_model // 4), d_model // 4)
            xbuf[:, cols] = jnp.dot(dmat[rows, :], hall[:, cols], preferred_element_type=F32).astype(BF16)

        def one_expert(k, _):
            i = g * d_group + k
            slot = lax.rem(i, n_gu)
            x = xbuf[pl.ds(pl.multiple_of(k * cap, cap), cap), :]
            g_copy(i).wait()
            u_copy(i).wait()
            gate_pre = jnp.dot(x, gbuf[slot], preferred_element_type=F32)
            up_pre = jnp.dot(x, ubuf[slot], preferred_element_type=F32)
            act = (gate_pre * jax.nn.sigmoid(gate_pre) * up_pre).astype(BF16)
            abuf[pl.ds(pl.multiple_of(i * cap, cap), cap), :] = act

            @pl.when(i + n_gu < n_local)
            def _():
                g_copy(i + n_gu).start()
                u_copy(i + n_gu).start()

            return 0

        lax.fori_loop(0, d_group, one_expert, 0)
        return 0

    lax.fori_loop(0, n_grp - 1, expert_group, 0)

    gate_l = lax.dot_general(hall[:, gate_cols], pick, NT, preferred_element_type=F32)
    lower = jnp.where((row_i > col_i) & same, 1.0, 0.0).astype(BF16)
    rank_l = jnp.dot(lower, jnp.where(gate_l > 0, 1.0, 0.0).astype(BF16), preferred_element_type=F32)
    shard_l = (lax.broadcasted_iota(jnp.int32, (n_rows, n_local), 0) // shard * (cap // n_ep)).astype(F32)
    key_l = jnp.where(gate_l > 0, rank_l + shard_l, -1.0).astype(BF16)
    gate_b = gate_l.astype(BF16)
    step = 256
    for c in range(n_local * cap // step):
        spread = (lax.broadcasted_iota(jnp.int32, (n_local, step), 0)
                  == (lax.broadcasted_iota(jnp.int32, (n_local, step), 1) + c * step) // cap).astype(BF16)
        key_x = jnp.dot(key_l, spread, preferred_element_type=F32)
        gate_x = jnp.dot(gate_b, spread, preferred_element_type=F32)
        lane = (lax.broadcasted_iota(jnp.int32, (n_rows, step), 1) % cap).astype(F32)
        cmat[:, pl.ds(c * step, step)] = jnp.where(key_x == lane, gate_x, 0.0).astype(BF16)

    lax.fori_loop(n_grp - 1, n_grp, expert_group, 0)

    def r_copy(j, d, block_sent, block_from, dev):
        rows = pl.ds(pl.multiple_of(block_sent * half, half), half)
        return pltpu.make_async_remote_copy(
            src_ref=pbuf.at[j, rows], dst_ref=rbuf.at[j, block_from], send_sem=r_send.at[j, d],
            recv_sem=r_recv.at[j, block_from], device_id=dev, device_id_type=MESH)

    def o_copy(j, block_t):
        return pltpu.make_async_remote_copy(
            src_ref=obuf.at[j, block_t], dst_ref=obuf.at[j, block_t], send_sem=o_send.at[j], recv_sem=o_recv.at[j],
            device_id={"tp": other_t, "ep": me_e}, device_id_type=MESH)

    def finish(j):
        cols = pl.ds(pl.multiple_of(j * d_cols, d_cols), d_cols)
        total = pbuf[j, my_rows, :].astype(F32)
        for d in range(1, n_dev):
            pid, dev = peer_of(d)
            r_copy(j, d, pid, pid, dev).wait_recv()
            total = total + rbuf[j, pid].astype(F32)
        obuf[j, me_t] = (x1buf[:, cols].astype(F32) + total).astype(BF16)
        o_copy(j, me_t).start()

    lag = 2

    def one_col(j, _):
        def one_part(g, _):
            q = j * n_grp + g
            slot = lax.rem(q, n_dr)
            d_copy(q).wait()
            for k in range(d_group):
                rows = pl.ds(pl.multiple_of((g * d_group + k) * cap, cap), cap)
                ybuf[rows, :] = jnp.dot(abuf[rows, :], dbuf[slot, k], preferred_element_type=F32).astype(BF16)

            @pl.when(q + n_dr < n_down)
            def _():
                d_copy(q + n_dr).start()

            return 0

        lax.fori_loop(0, n_grp, one_part, 0)
        pbuf[j] = jnp.dot(cmat[...], ybuf[...], preferred_element_type=F32).astype(BF16)
        for d in range(1, n_dev):
            pid, dev = peer_of(d)
            r_copy(j, d, pid, me, dev).start()

        @pl.when(j >= lag)
        def _():
            finish(j - lag)

        return 0

    lax.fori_loop(0, n_col, one_col, 0)
    for j in range(n_col - lag, n_col):
        finish(j)

    def drain(j, _):
        for d in range(1, n_dev):
            pid, dev = peer_of(d)
            r_copy(j, d, pid, me, dev).wait_send()
        o_copy(j, me_t).wait_send()
        return 0

    lax.fori_loop(0, n_col, drain, 0)
    for d in range(1, n_dev):
        _, dev = peer_of(d)
        h_copy(d, me, dev).wait_send()
    for j in range(n_col):
        o_copy(j, other_t).wait_recv()
        for t in range(n_tp):
            out_ref[t * half:(t + 1) * half, j * d_cols:(j + 1) * d_cols] = obuf[j, t]


def moe_call(n_tp, n_ep, part, hidden, b_out, ln_scale, ln_bias, w_router, ids_t, w_gate, w_up, w_down):
    n_b, d_model = hidden.shape
    n_local, _, width = w_gate.shape
    n_exp = n_local * n_ep
    n_rows = n_b * n_ep
    n_dev = n_tp * n_ep
    half = n_b // n_tp
    cap = 32
    n_gu, n_dr, d_group, d_cols = 9, 12, 8, 256
    n_col = d_model // d_cols
    vmem = pl.BlockSpec(memory_space=pltpu.VMEM)
    hbm = pl.BlockSpec(memory_space=pl.ANY)
    dma = pltpu.SemaphoreType.DMA
    return pl.pallas_call(
        functools.partial(moe_kernel, n_tp, n_ep),
        out_shape=jax.ShapeDtypeStruct((n_b, d_model), BF16),
        in_specs=[vmem] * 7 + [hbm] * 3,
        out_specs=vmem,
        scratch_shapes=[
            pltpu.VMEM((n_gu, d_model, width), BF16),
            pltpu.VMEM((n_gu, d_model, width), BF16),
            pltpu.VMEM((n_dr, d_group, width, d_cols), BF16),
            pltpu.VMEM((n_rows, d_model + n_exp), BF16),
            pltpu.VMEM((half, d_model), BF16),
            pltpu.VMEM((half, d_model), BF16),
            pltpu.VMEM((n_local * cap, n_rows), BF16),
            pltpu.VMEM((n_rows, n_local * cap), BF16),
            pltpu.VMEM((d_group * cap, d_model), BF16),
            pltpu.VMEM((n_local * cap, width), BF16),
            pltpu.VMEM((n_local * cap, d_cols), BF16),
            pltpu.VMEM((n_col, n_rows, d_cols), BF16),
            pltpu.VMEM((n_col, n_dev, half, d_cols), BF16),
            pltpu.VMEM((n_col, n_tp, half, d_cols), BF16),
            dma((n_gu,)), dma((n_gu,)), dma((n_dr,)), dma, dma, dma((n_dev,)), dma((n_dev,)),
            dma((n_col, n_dev)), dma((n_col, n_dev)), dma((n_col,)), dma((n_col,)),
        ],
        compiler_params=pltpu.CompilerParams(
            collective_id=0, has_side_effects=True, vmem_limit_bytes=67043328),
        name="moe",
    )(part, hidden, b_out, ln_scale, ln_bias, w_router, ids_t, w_gate, w_up, w_down)


def solution(mesh):
    n_tp, n_ep = mesh.shape['tp'], mesh.shape['ep']
    token_rows = P(('dp', 'ep'), None)
    token_vec = P(('dp', 'ep'))
    cache_spec = P(('dp', 'ep'), None, 'tp', None)
    expert_in = P('ep', None, 'tp')
    expert_down = P('ep', 'tp', None)

    def device_step(hidden, seq_lens, rope_cos, rope_sin, ln1_scale, ln1_bias, w_qkv, b_qkv, w_out, b_out, k_cache, v_cache, ln2_scale, ln2_bias, w_router, expert_ids, w_gate, w_up, w_down):
        n_b, s_max, n_groups, head = k_cache.shape
        k_rows = k_cache.reshape(n_b, s_max * n_groups, head)
        v_rows = v_cache.reshape(n_b, s_max * n_groups, head)
        part, k_out, v_out = attention_call(
            hidden, seq_lens, rope_cos, rope_sin, ln1_scale[None], ln1_bias[None], w_qkv, b_qkv[None], w_out, k_rows, v_rows)
        hidden_out = moe_call(
            n_tp, n_ep, part, hidden, b_out[None], ln2_scale[None], ln2_bias[None], w_router, expert_ids.T, w_gate, w_up, w_down)
        return hidden_out, k_out.reshape(k_cache.shape), v_out.reshape(v_cache.shape)

    in_specs = (token_rows, token_vec, token_rows, token_rows, P(), P(), P(None, 'tp'), P('tp'), P('tp', None), P(), cache_spec, cache_spec, P(), P(), P(), token_rows, expert_in, expert_in, expert_down)
    return jax.shard_map(device_step, mesh=mesh, in_specs=in_specs, out_specs=(token_rows, cache_spec, cache_spec), check_vma=False)
```

time: 356 us -> 99.5 us (0.28)
  waiting for transfers between devices: 164 us -> 0 us
  Pallas kernels: 0 us -> 89.1 us
  matrix products: 88.2 us -> 0 us
  blocking collectives: 51.5 us -> 0 us
  other arithmetic: 20.9 us -> 0 us
  between operations: 14.4 us -> 0.65 us
  starting transfers between devices: 5.16 us -> 0 us
    psum x2 -> x0, waiting for transfers between devices: 121 us -> none  [the longest x1 101 us: device_step(): expert_out = lax.psum(down_part, 'tp')]
    pallas_call x0 -> x2, Pallas kernels: none -> 89.1 us  [the longest x1 71.5 us: moe_call(): pl.pallas_call(functools.partial(moe_kernel, n_tp, n_ep), out_shape=jax.S...]
    dot_general x9 -> x0, matrix products: 83.5 us -> none  [the longest x1 20.5 us: expert_ffn(): jnp.einsum('escf,efd->escd', hidden_act, w_down, preferred_element_type=j...]
    all_to_all x1 -> x0, blocking collectives: 51.5 us -> none  [device_step(): lax.all_to_all(outgoing, 'ep', 0, 0, tiled=True)]
    all_to_all x1 -> x0, waiting for transfers between devices: 43 us -> none  [device_step(): lax.all_to_all(expert_out, 'ep', 1, 0, tiled=True)]
    select_n x2 -> x0, other arithmetic: 13.8 us -> none  [the longest x1 13.8 us: attention_part(): k_cache_out = jnp.where(write_mask, key_new[:, None], k_cache)]
    broadcast_in_dim x1 -> x6, local copies, waits for them, and re-layouts: 0.04 us -> 7.72 us  [the longest x1 1.29 us: device_step(): ln2_scale[None]]
    all_to_all x1 -> x0, starting transfers between devices: 5.08 us -> none  [device_step(): lax.all_to_all(expert_out, 'ep', 1, 0, tiled=True)]
  transfers between devices with their start and end apart: 3 -> 0, of which waited for: 3 -> 0; matrix products, arithmetic and copies ran while one was open for 1% -> 0% of each run, Pallas kernels for 0% -> 0%
where the time goes in v1:
time: 99.5 us; the launch traced here: 99.1 us
  Pallas kernels  89.1 us (90%)
  local copies, waits for them, and re-layouts  9.39 us (9%)
    pallas_call x1, Pallas kernels, moe_call(): pl.pallas_call(functools.partial(moe_kernel, n_tp, n_ep), out_shape=jax.S...  71.5 us
    pallas_call x1, Pallas kernels, attention_call(): pl.pallas_call(attn_kernel, out_shape=(jax.ShapeDtypeStruct((n_b, d_model...  17.6 us

profile of v1, /device:TPU:0, one launch (start us, length us, event | category | flops | bytes accessed | tf_op | source)
XLA Modules:
  0.0 99.1 jit_solution(12074461510966374675)
XLA Ops:
  0.6 1.3 %broadcast_in_dim.18.lns_ref = bf16[1,2048]{1,0:T(2,128)(2,1)} reshape(bf16[2048]{0:T(1024)(128)(2,1)} %param.23) | data formatting | bytes 8192 | tf_op jit(solution)/shard_map/broadcast_in_dim | solution.py:458
  1.9 1.3 %broadcast_in_dim.19.lnb_ref = bf16[1,2048]{1,0:T(2,128)(2,1)} reshape(bf16[2048]{0:T(1024)(128)(2,1)} %param.24) | data formatting | bytes 8192 | tf_op jit(solution)/shard_map/broadcast_in_dim | solution.py:458
  3.2 1.3 %broadcast_in_dim.21.bout_ref = bf16[1,2048]{1,0:T(2,128)(2,1)} reshape(bf16[2048]{0:T(1024)(128)(2,1)} %param.28) | data formatting | bytes 8192 | tf_op jit(solution)/shard_map/broadcast_in_dim | solution.py:460
  4.5 1.3 %broadcast_in_dim.22.lns_ref = bf16[1,2048]{1,0:T(2,128)(2,1)} reshape(bf16[2048]{0:T(1024)(128)(2,1)} %param.31) | data formatting | bytes 8192 | tf_op jit(solution)/shard_map/broadcast_in_dim | solution.py:460
  5.8 1.3 %broadcast_in_dim.23.lnb_ref = bf16[1,2048]{1,0:T(2,128)(2,1)} reshape(bf16[2048]{0:T(1024)(128)(2,1)} %param.32) | data formatting | bytes 8192 | tf_op jit(solution)/shard_map/broadcast_in_dim | solution.py:460
  7.1 1.3 %broadcast_in_dim.20.bq_ref = bf16[1,2560]{1,0:T(2,128)(2,1)} reshape(bf16[2560]{0:T(1024)(128)(2,1)} %param.26) | data formatting | bytes 10240 | tf_op jit(solution)/shard_map/broadcast_in_dim | solution.py:458
  8.4 17.6 %attn.1 = (bf16[64,2048]{1,0:T(8,128)(2,1)}, bf16[64,256,128]{2,1,0:T(8,128)(2,1)}, bf16[64,256,128]{2,1,0:T(8,128)(2,1)}) custom-call(s32[64]{0:T(128)} %seq_ref.1, bf16[64,2048]{1,0:T(8,128)(2,1)} %hid_ref.3, f32[64,64]{1,0:T(8,128)} %cos_ref.1, f32[64,64]{1,0:T(8,128)} %sin_ref.1, bf16[1,2048]{1,0:T(2,128)(2,1)} %broadcast_in_dim.18.lns_ref, ...), custom_call_target="tpu_custom_call" | custom-call | tf_op jit(solution)/shard_map/attn/pallas_call | solution.py:145
  26.0 71.5 %moe.1 = bf16[64,2048]{1,0:T(8,128)(2,1)} custom-call(bf16[64,2048]{1,0:T(8,128)(2,1)} %get-tuple-element.6.part_ref, bf16[64,2048]{1,0:T(8,128)(2,1)} %hid_ref.3, bf16[1,2048]{1,0:T(2,128)(2,1)} %broadcast_in_dim.21.bout_ref, bf16[1,2048]{1,0:T(2,128)(2,1)} %broadcast_in_dim.22.lns_ref, bf16[1,2048]{1,0:T(2,128)(2,1)} %broadcast_in_dim.23.lnb_ref, ...), custom_call_target="tpu_custom_call" | custom-call | tf_op jit(solution)/shard_map/moe/pallas_call | solution.py:416
  97.5 1.7 %copy.23 = bf16[64,2048]{1,0:T(8,128)(2,1)} copy(bf16[64,2048]{1,0:T(8,128)(2,1)} %moe.1) | data formatting | bytes 524288

commit v2 on v1

--- a/solution.py
+++ b/solution.py
@@ -14,12 +14,23 @@
 NT = (((1,), (1,)), ((), ()))
 
 
+def as_row(vec):
+    return vec.astype(F32).reshape(1, vec.shape[0])
+
+
 def layer_norm(vals_f32, scale, bias):
     row_mean = jnp.mean(vals_f32, axis=-1, keepdims=True)
     centered = vals_f32 - row_mean
     row_var = jnp.mean(centered * centered, axis=-1, keepdims=True)
     normed = centered * lax.rsqrt(row_var + EPS)
-    return (normed * scale.astype(F32) + bias.astype(F32)).astype(BF16)
+    return (normed * as_row(scale) + as_row(bias)).astype(BF16)
+
+
+def load_all(sources, targets, sems):
+    copies = [pltpu.make_async_copy(src, dst, sems.at[i]) for i, (src, dst) in enumerate(zip(sources, targets))]
+    for copy in copies:
+        copy.start()
+    return copies
 
 
 def attn_kernel(seq_ref, hid_ref, cos_ref, sin_ref, lns_ref, lnb_ref, bq_ref, wq_hbm, kc_hbm, vc_hbm, wo_hbm,
@@ -31,7 +42,7 @@
     n_wo, _, wo_cols = wo_buf.shape
     rows = kbuf.shape[1]
     heads = qs.shape[0] // n_b
-    chunk = 8
+    chunk = 16
     n_chunk = n_b // chunk
 
     def wq_copy(n):
@@ -52,13 +63,14 @@
     def vo_copy(c):
         return pltpu.make_async_copy(vbuf.at[pl.ds(c * chunk, chunk)], vo_hbm.at[pl.ds(c * chunk, chunk)], vo_sem.at[c])
 
-    for n in range(n_wq):
-        wq_copy(n).start()
-    for c in range(n_chunk):
-        k_copy(c).start()
-        v_copy(c).start()
+    stages = [[] for _ in range(n_wq)]
+    first = [wq_copy(n) for n in range(n_wq)] + [k_copy(0), v_copy(0)]
+    for c in range(1, n_chunk):
+        stages[min(c - 1, n_wq - 1)] += [k_copy(c), v_copy(c)]
     for n in range(n_wo):
-        wo_copy(n).start()
+        stages[min(n_chunk - 1 + n // 2, n_wq - 1)].append(wo_copy(n))
+    for copy in first:
+        copy.start()
 
     hbuf[...] = layer_norm(hid_ref[...].astype(F32), lns_ref[...], lnb_ref[...])
     cos2 = jnp.concatenate([cos_ref[...], cos_ref[...]], axis=1)
@@ -66,8 +78,10 @@
     per_group = heads // 2 + 2
     for n in range(n_wq):
         wq_copy(n).wait()
+        for copy in stages[n]:
+            copy.start()
         cols = pl.ds(n * wq_cols, wq_cols)
-        qkv = jnp.dot(hbuf[...], wq_buf[n], preferred_element_type=F32) + bq_ref[:, cols].astype(F32)
+        qkv = jnp.dot(hbuf[...], wq_buf[n], preferred_element_type=F32) + as_row(bq_ref[cols])
         qkv = qkv.astype(BF16).astype(F32)
         for i in range(wq_cols // 128):
             g, j = divmod(n * (wq_cols // 128) + i, per_group)
@@ -162,22 +176,24 @@
             pltpu.VMEM((n_b * 2, 128), F32),
             pltpu.VMEM((n_b * heads, 128), F32),
             pltpu.VMEM((n_b, heads * 128), BF16),
-            dma((n_wq,)), dma((n_b // 8,)), dma((n_b // 8,)), dma((n_wo,)), dma((n_b // 8,)), dma((n_b // 8,)),
+            dma((n_wq,)), dma((n_b // 16,)), dma((n_b // 16,)), dma((n_wo,)), dma((n_b // 16,)), dma((n_b // 16,)),
         ],
         compiler_params=pltpu.CompilerParams(vmem_limit_bytes=60 * 1024 * 1024),
         name="attn",
     )(seq_lens, hidden, rope_cos, rope_sin, ln_scale, ln_bias, b_qkv, w_qkv, k_rows, v_rows, w_out)
 
 
-def moe_kernel(n_tp, n_ep, part_ref, hid_ref, bout_ref, lns_ref, lnb_ref, wr_ref, ids_ref, wg_hbm, wu_hbm, wd_hbm,
+def moe_kernel(n_tp, n_ep, part_in, hid_in, bout_in, lns_in, lnb_in, wr_in, ids_in, wg_hbm, wu_hbm, wd_hbm,
                out_ref,
-               gbuf, ubuf, dbuf, hall, arx, x1buf, dmat, cmat, xbuf, abuf, ybuf, pbuf, rbuf, obuf,
+               part_ref, hid_ref, bout_ref, lns_ref, lnb_ref, wr_ref, ids_ref, in_sem,
+               gubuf, dbuf, hall, arx, x1buf, dmat, cmat, xbuf, abuf, ybuf, pbuf, rbuf, obuf,
                gsem, usem, dsem, a_send, a_recv, h_send, h_recv, r_send, r_recv, o_send, o_recv):
     me_t = lax.axis_index("tp")
     me_e = lax.axis_index("ep")
     n_dev = n_tp * n_ep
     me = me_e * n_tp + me_t
-    n_gu, d_model, width = gbuf.shape
+    n_gu, d_model, _ = gubuf.shape
+    width = wg_hbm.shape[2]
     n_dr, d_group, _, d_cols = dbuf.shape
     n_local = wg_hbm.shape[0]
     n_exp = n_local * n_ep
@@ -188,6 +204,9 @@
     n_col = d_model // d_cols
     n_grp = n_local // d_group
     n_down = n_col * n_grp
+    x_group = xbuf.shape[0] // cap
+    n_xg = n_local // x_group
+    n_unroll = 2
 
     def peer_of(d):
         pid = lax.rem(me + d, n_dev)
@@ -195,11 +214,11 @@
 
     def g_copy(i):
         slot = lax.rem(i, n_gu)
-        return pltpu.make_async_copy(wg_hbm.at[i], gbuf.at[slot], gsem.at[slot])
+        return pltpu.make_async_copy(wg_hbm.at[i], gubuf.at[slot, :, pl.ds(0, width)], gsem.at[slot])
 
     def u_copy(i):
         slot = lax.rem(i, n_gu)
-        return pltpu.make_async_copy(wu_hbm.at[i], ubuf.at[slot], usem.at[slot])
+        return pltpu.make_async_copy(wu_hbm.at[i], gubuf.at[slot, :, pl.ds(width, width)], usem.at[slot])
 
     def d_copy(q):
         slot = lax.rem(q, n_dr)
@@ -217,20 +236,48 @@
         d_copy(q).start()
         return 0
 
-    lax.fori_loop(0, n_gu, first_gu, 0)
-    lax.fori_loop(0, n_dr, first_d, 0)
-
     barrier = pltpu.get_barrier_semaphore()
     for d in range(1, n_dev):
         _, dev = peer_of(d)
         pl.semaphore_signal(barrier, inc=1, device_id=dev, device_id_type=MESH)
+    small = load_all((part_in, hid_in, bout_in, lns_in, lnb_in, wr_in, ids_in),
+                     (part_ref, hid_ref, bout_ref, lns_ref, lnb_ref, wr_ref, ids_ref), in_sem)
+    lax.fori_loop(0, n_gu, first_gu, 0)
+    lax.fori_loop(0, n_dr, first_d, 0)
+    for copy in small:
+        copy.wait()
     pl.semaphore_wait(barrier, n_dev - 1)
 
     other_t = 1 - me_t
-    a_copy = pltpu.make_async_remote_copy(
-        src_ref=part_ref.at[pl.ds(pl.multiple_of(other_t * half, half), half)], dst_ref=arx,
-        send_sem=a_send, recv_sem=a_recv, device_id={"tp": other_t, "ep": me_e}, device_id_type=MESH)
-    a_copy.start()
+    core = lax.rem(me_e, 2)
+    sib_e = me_e + 1 - 2 * core
+    far_e = lax.rem(me_e + 2, n_ep)
+    near_dev = {"tp": me_t, "ep": sib_e}
+    n_sub = a_send.shape[0]
+    sub = half // n_sub
+
+    def a_copy(s):
+        rows = pl.ds(pl.multiple_of(other_t * half + s * sub, sub), sub)
+        return pltpu.make_async_remote_copy(
+            src_ref=part_ref.at[rows], dst_ref=arx.at[pl.ds(s * sub, sub)], send_sem=a_send.at[s],
+            recv_sem=a_recv.at[s], device_id={"tp": other_t, "ep": me_e}, device_id_type=MESH)
+
+    for s in range(n_sub):
+        a_copy(s).start()
+
+    def h_copy(step, s, block_e, block_t, dev):
+        block = block_e * n_tp + block_t
+        rows = pl.ds(pl.multiple_of(block * half + s * sub, sub), sub)
+        return pltpu.make_async_remote_copy(
+            src_ref=hall.at[rows], dst_ref=hall.at[rows], send_sem=h_send.at[step, s], recv_sem=h_recv.at[block, s],
+            device_id=dev, device_id_type=MESH)
+
+    far_dev = {"tp": me_t, "ep": far_e}
+    side_dev = {"tp": other_t, "ep": me_e}
+    diag_dev = {"tp": other_t, "ep": far_e}
+    sends = (
+        (0, me_e, me_t, far_dev), (1, me_e, me_t, side_dev), (2, me_e, me_t, near_dev), (3, me_e, me_t, diag_dev),
+        (4, far_e, me_t, near_dev), (5, me_e, other_t, near_dev), (6, far_e, other_t, near_dev))
 
     picked_t = jnp.zeros((n_exp, shard), F32)
     exp_row = lax.broadcasted_iota(jnp.int32, (n_exp, shard), 0)
@@ -240,32 +287,34 @@
            == lax.broadcasted_iota(jnp.int32, (half, shard), 0) + me_t * half).astype(BF16)
     picked = lax.dot_general(sel, picked_t.astype(BF16), NT, preferred_element_type=F32)
 
-    mine = pl.ds(pl.multiple_of(me_t * half, half), half)
-    a_copy.wait()
-    attn = part_ref[mine, :].astype(F32) + arx[...].astype(F32)
-    x1 = (hid_ref[mine, :].astype(F32) + attn + bout_ref[...].astype(F32)).astype(BF16)
-    x1buf[...] = x1
-    h2 = layer_norm(x1.astype(F32), lns_ref[...], lnb_ref[...])
     my_rows = pl.ds(pl.multiple_of(me * half, half), half)
-    hall[my_rows, pl.ds(0, d_model)] = h2
-    logits = jnp.dot(h2, wr_ref[...], preferred_element_type=F32)
-    logits = jnp.where(picked > 0.5, logits, -jnp.inf)
-    e = jnp.exp(logits - jnp.max(logits, axis=-1, keepdims=True))
-    gates = e / jnp.sum(e, axis=-1, keepdims=True)
-    hall[my_rows, pl.ds(d_model, n_exp)] = gates.astype(BF16)
-
-    def h_copy(d, block, dev):
-        rows = pl.ds(pl.multiple_of(block * half, half), half)
-        return pltpu.make_async_remote_copy(
-            src_ref=hall.at[rows], dst_ref=hall.at[rows], send_sem=h_send.at[d], recv_sem=h_recv.at[block],
-            device_id=dev, device_id_type=MESH)
-
-    for d in range(1, n_dev):
-        _, dev = peer_of(d)
-        h_copy(d, me, dev).start()
-    for d in range(1, n_dev):
-        pid, dev = peer_of(d)
-        h_copy(d, pid, dev).wait_recv()
+    for s in range(n_sub):
+        rows = pl.ds(pl.multiple_of(me_t * half + s * sub, sub), sub)
+        attn = part_ref[rows, :].astype(F32)
+        base = hid_ref[rows, :].astype(F32)
+        a_copy(s).wait_recv()
+        attn = attn + arx[s * sub:(s + 1) * sub, :].astype(F32)
+        x1 = (base + attn + as_row(bout_ref[...])).astype(BF16)
+        x1buf[s * sub:(s + 1) * sub, :] = x1
+        h2 = layer_norm(x1.astype(F32), lns_ref[...], lnb_ref[...])
+        hall_rows = pl.ds(pl.multiple_of(me * half + s * sub, sub), sub)
+        hall[hall_rows, pl.ds(0, d_model)] = h2
+        logits = jnp.dot(h2, wr_ref[...], preferred_element_type=F32)
+        logits = jnp.where(picked[s * sub:(s + 1) * sub, :] > 0.5, logits, -jnp.inf)
+        e = jnp.exp(logits - jnp.max(logits, axis=-1, keepdims=True))
+        gates = e / jnp.sum(e, axis=-1, keepdims=True)
+        hall[hall_rows, pl.ds(d_model, n_exp)] = gates.astype(BF16)
+        for step, block_e, block_t, dev in sends[:4]:
+            h_copy(step, s, block_e, block_t, dev).start()
+
+    for s in range(n_sub):
+        for step, block_e, block_t, dev in sends[4:]:
+            h_copy(0, s, block_e, block_t, near_dev).wait_recv()
+            h_copy(step, s, block_e, block_t, dev).start()
+    for s in range(n_sub):
+        for block_e, block_t in ((sib_e, me_t), (sib_e, other_t), (lax.rem(sib_e + 2, n_ep), me_t),
+                                 (lax.rem(sib_e + 2, n_ep), other_t)):
+            h_copy(0, s, block_e, block_t, near_dev).wait_recv()
 
     gate_cols = pl.ds(d_model, n_exp)
     pick = (lax.broadcasted_iota(jnp.int32, (n_local, n_exp), 1)
@@ -284,33 +333,38 @@
         dmat[i * cap:(i + 1) * cap, :] = jnp.where(key_t[i:i + 1, :] == slot_i, 1.0, 0.0).astype(BF16)
 
     def expert_group(g, _):
-        rows = pl.ds(pl.multiple_of(g * d_group * cap, d_group * cap), d_group * cap)
+        rows = pl.ds(pl.multiple_of(g * x_group * cap, x_group * cap), x_group * cap)
         for c in range(4):
             cols = pl.ds(c * (d_model // 4), d_model // 4)
             xbuf[:, cols] = jnp.dot(dmat[rows, :], hall[:, cols], preferred_element_type=F32).astype(BF16)
 
-        def one_expert(k, _):
-            i = g * d_group + k
-            slot = lax.rem(i, n_gu)
-            x = xbuf[pl.ds(pl.multiple_of(k * cap, cap), cap), :]
-            g_copy(i).wait()
-            u_copy(i).wait()
-            gate_pre = jnp.dot(x, gbuf[slot], preferred_element_type=F32)
-            up_pre = jnp.dot(x, ubuf[slot], preferred_element_type=F32)
-            act = (gate_pre * jax.nn.sigmoid(gate_pre) * up_pre).astype(BF16)
-            abuf[pl.ds(pl.multiple_of(i * cap, cap), cap), :] = act
-
-            @pl.when(i + n_gu < n_local)
-            def _():
-                g_copy(i + n_gu).start()
-                u_copy(i + n_gu).start()
+        def some_experts(k, _):
+            first = g * x_group + k * n_unroll
+            for u in range(n_unroll):
+                g_copy(first + u).wait()
+                u_copy(first + u).wait()
+            both = []
+            for u in range(n_unroll):
+                x = xbuf[pl.ds(pl.multiple_of((k * n_unroll + u) * cap, cap), cap), :]
+                both.append(jnp.dot(x, gubuf[lax.rem(first + u, n_gu)], preferred_element_type=F32))
+            for u in range(n_unroll):
+                gate_pre, up_pre = both[u][:, :width], both[u][:, width:]
+                act = (gate_pre * jax.nn.sigmoid(gate_pre) * up_pre).astype(BF16)
+                abuf[pl.ds(pl.multiple_of((first + u) * cap, cap), cap), :] = act
+            for u in range(n_unroll):
+                i = first + u
+
+                @pl.when(i + n_gu < n_local)
+                def _():
+                    g_copy(i + n_gu).start()
+                    u_copy(i + n_gu).start()
 
             return 0
 
-        lax.fori_loop(0, d_group, one_expert, 0)
+        lax.fori_loop(0, x_group // n_unroll, some_experts, 0)
         return 0
 
-    lax.fori_loop(0, n_grp - 1, expert_group, 0)
+    lax.fori_loop(0, n_xg - 1, expert_group, 0)
 
     gate_l = lax.dot_general(hall[:, gate_cols], pick, NT, preferred_element_type=F32)
     lower = jnp.where((row_i > col_i) & same, 1.0, 0.0).astype(BF16)
@@ -327,7 +381,7 @@
         lane = (lax.broadcasted_iota(jnp.int32, (n_rows, step), 1) % cap).astype(F32)
         cmat[:, pl.ds(c * step, step)] = jnp.where(key_x == lane, gate_x, 0.0).astype(BF16)
 
-    lax.fori_loop(n_grp - 1, n_grp, expert_group, 0)
+    lax.fori_loop(n_xg - 1, n_xg, expert_group, 0)
 
     def r_copy(j, d, block_sent, block_from, dev):
         rows = pl.ds(pl.multiple_of(block_sent * half, half), half)
@@ -357,9 +411,20 @@
             q = j * n_grp + g
             slot = lax.rem(q, n_dr)
             d_copy(q).wait()
-            for k in range(d_group):
-                rows = pl.ds(pl.multiple_of((g * d_group + k) * cap, cap), cap)
-                ybuf[rows, :] = jnp.dot(abuf[rows, :], dbuf[slot, k], preferred_element_type=F32).astype(BF16)
+            main = width // 256 * 256
+            rest = width - main
+            pad = jnp.zeros((cap, rest), BF16)
+            for k in range(0, d_group, 2):
+                rows = [pl.ds(pl.multiple_of((g * d_group + k + u) * cap, cap), cap) for u in range(2)]
+                acts = [abuf[rows[u], :] for u in range(2)]
+                ends = jnp.concatenate([
+                    jnp.concatenate([acts[0][:, main:], pad], axis=1),
+                    jnp.concatenate([pad, acts[1][:, main:]], axis=1)], axis=0)
+                end_w = jnp.concatenate([dbuf[slot, k, main:, :], dbuf[slot, k + 1, main:, :]], axis=0)
+                tail = jnp.dot(ends, end_w, preferred_element_type=F32)
+                for u in range(2):
+                    y = jnp.dot(acts[u][:, :main], dbuf[slot, k + u, :main, :], preferred_element_type=F32)
+                    ybuf[rows[u], :] = (y + tail[u * cap:(u + 1) * cap]).astype(BF16)
 
             @pl.when(q + n_dr < n_down)
             def _():
@@ -368,7 +433,9 @@
             return 0
 
         lax.fori_loop(0, n_grp, one_part, 0)
-        pbuf[j] = jnp.dot(cmat[...], ybuf[...], preferred_element_type=F32).astype(BF16)
+        for u in range(2):
+            part_rows = slice(u * n_rows // 2, (u + 1) * n_rows // 2)
+            pbuf[j, part_rows, :] = jnp.dot(cmat[part_rows, :], ybuf[...], preferred_element_type=F32).astype(BF16)
         for d in range(1, n_dev):
             pid, dev = peer_of(d)
             r_copy(j, d, pid, me, dev).start()
@@ -391,9 +458,10 @@
         return 0
 
     lax.fori_loop(0, n_col, drain, 0)
-    for d in range(1, n_dev):
-        _, dev = peer_of(d)
-        h_copy(d, me, dev).wait_send()
+    for s in range(n_sub):
+        a_copy(s).wait_send()
+        for step, block_e, block_t, dev in sends:
+            h_copy(step, s, block_e, block_t, dev).wait_send()
     for j in range(n_col):
         o_copy(j, other_t).wait_recv()
         for t in range(n_tp):
@@ -408,7 +476,8 @@
     n_dev = n_tp * n_ep
     half = n_b // n_tp
     cap = 32
-    n_gu, n_dr, d_group, d_cols = 9, 12, 8, 256
+    n_gu, n_dr, d_group, d_cols = 12, 4, 16, 256
+    n_sub = 2
     n_col = d_model // d_cols
     vmem = pl.BlockSpec(memory_space=pltpu.VMEM)
     hbm = pl.BlockSpec(memory_space=pl.ANY)
@@ -416,24 +485,24 @@
     return pl.pallas_call(
         functools.partial(moe_kernel, n_tp, n_ep),
         out_shape=jax.ShapeDtypeStruct((n_b, d_model), BF16),
-        in_specs=[vmem] * 7 + [hbm] * 3,
+        in_specs=[hbm] * 10,
         out_specs=vmem,
-        scratch_shapes=[
-            pltpu.VMEM((n_gu, d_model, width), BF16),
-            pltpu.VMEM((n_gu, d_model, width), BF16),
+        scratch_shapes=[pltpu.VMEM(x.shape, x.dtype) for x in (part, hidden, b_out, ln_scale, ln_bias, w_router, ids_t)] + [
+            dma((7,)),
+            pltpu.VMEM((n_gu, d_model, 2 * width), BF16),
             pltpu.VMEM((n_dr, d_group, width, d_cols), BF16),
             pltpu.VMEM((n_rows, d_model + n_exp), BF16),
             pltpu.VMEM((half, d_model), BF16),
             pltpu.VMEM((half, d_model), BF16),
             pltpu.VMEM((n_local * cap, n_rows), BF16),
             pltpu.VMEM((n_rows, n_local * cap), BF16),
-            pltpu.VMEM((d_group * cap, d_model), BF16),
+            pltpu.VMEM((8 * cap, d_model), BF16),
             pltpu.VMEM((n_local * cap, width), BF16),
             pltpu.VMEM((n_local * cap, d_cols), BF16),
             pltpu.VMEM((n_col, n_rows, d_cols), BF16),
             pltpu.VMEM((n_col, n_dev, half, d_cols), BF16),
             pltpu.VMEM((n_col, n_tp, half, d_cols), BF16),
-            dma((n_gu,)), dma((n_gu,)), dma((n_dr,)), dma, dma, dma((n_dev,)), dma((n_dev,)),
+            dma((n_gu,)), dma((n_gu,)), dma((n_dr,)), dma((n_sub,)), dma((n_sub,)), dma((7, n_sub)), dma((n_dev, n_sub)),
             dma((n_col, n_dev)), dma((n_col, n_dev)), dma((n_col,)), dma((n_col,)),
         ],
         compiler_params=pltpu.CompilerParams(
@@ -455,9 +524,9 @@
         k_rows = k_cache.reshape(n_b, s_max * n_groups, head)
         v_rows = v_cache.reshape(n_b, s_max * n_groups, head)
         part, k_out, v_out = attention_call(
-            hidden, seq_lens, rope_cos, rope_sin, ln1_scale[None], ln1_bias[None], w_qkv, b_qkv[None], w_out, k_rows, v_rows)
+            hidden, seq_lens, rope_cos, rope_sin, ln1_scale, ln1_bias, w_qkv, b_qkv, w_out, k_rows, v_rows)
         hidden_out = moe_call(
-            n_tp, n_ep, part, hidden, b_out[None], ln2_scale[None], ln2_bias[None], w_router, expert_ids.T, w_gate, w_up, w_down)
+            n_tp, n_ep, part, hidden, b_out, ln2_scale, ln2_bias, w_router, expert_ids.T, w_gate, w_up, w_down)
         return hidden_out, k_out.reshape(k_cache.shape), v_out.reshape(v_cache.shape)
 
     in_specs = (token_rows, token_vec, token_rows, token_rows, P(), P(), P(None, 'tp'), P('tp'), P('tp', None), P(), cache_spec, cache_spec, P(), P(), P(), token_rows, expert_in, expert_in, expert_down)

time: 99.5 us -> 78.8 us (0.79)
  Pallas kernels: 89.1 us -> 76.3 us
  local copies, waits for them, and re-layouts: 9.39 us -> 1.67 us
    pallas_call x1, Pallas kernels: 71.5 us -> 61.9 us  [moe_call(): pl.pallas_call(functools.partial(moe_kernel, n_tp, n_ep), out_shape=jax.S...]
    broadcast_in_dim x6 -> x0, local copies, waits for them, and re-layouts: 7.72 us -> none  [the longest x1 1.29 us: device_step(): ln2_scale[None]]
    pallas_call x1, Pallas kernels: 17.6 us -> 14.5 us  [attention_call(): pl.pallas_call(attn_kernel, out_shape=(jax.ShapeDtypeStruct((n_b, d_model...]
where the time goes in v2:
time: 78.8 us; the launch traced here: 78.7 us
  Pallas kernels  76.3 us (97%)
  local copies, waits for them, and re-layouts  1.67 us (2%)
    pallas_call x1, Pallas kernels, moe_call(): pl.pallas_call(functools.partial(moe_kernel, n_tp, n_ep), out_shape=jax.S...  61.9 us
    pallas_call x1, Pallas kernels, attention_call(): pl.pallas_call(attn_kernel, out_shape=(jax.ShapeDtypeStruct((n_b, d_model...  14.5 us
    unnamed x1, local copies, waits for them, and re-layouts  1.67 us

profile of v2, /device:TPU:0, one launch (start us, length us, event | category | flops | bytes accessed | tf_op | source)
XLA Modules:
  0.0 78.7 jit_solution(14617007915330061459)
XLA Ops:
  0.6 14.5 %attn.1 = (bf16[64,2048]{1,0:T(8,128)(2,1)}, bf16[64,256,128]{2,1,0:T(8,128)(2,1)}, bf16[64,256,128]{2,1,0:T(8,128)(2,1)}) custom-call(s32[64]{0:T(128)} %seq_ref.1, bf16[64,2048]{1,0:T(8,128)(2,1)} %hid_in.1, f32[64,64]{1,0:T(8,128)} %cos_ref.1, f32[64,64]{1,0:T(8,128)} %sin_ref.1, bf16[2048]{0:T(1024)(128)(2,1)} %lns_ref.1, bf16[2048]{0:T(1024)(128)(2,1)} %lnb_ref.1, ...), custom_call_target="tpu_custom_call" | custom-call | tf_op jit(solution)/shard_map/attn/pallas_call | solution.py:159
  15.1 61.9 %moe.1 = bf16[64,2048]{1,0:T(8,128)(2,1)} custom-call(bf16[64,2048]{1,0:T(8,128)(2,1)} %get-tuple-element.6.part_in, bf16[64,2048]{1,0:T(8,128)(2,1)} %hid_in.1, bf16[2048]{0:T(1024)(128)(2,1)} %bout_in.1, bf16[2048]{0:T(1024)(128)(2,1)} %lns_in.1, bf16[2048]{0:T(1024)(128)(2,1)} %lnb_in.1, bf16[2048,128]{1,0:T(8,128)(2,1)} %wr_in.1, s32[8,64]{1,0:T(8,128)} %bitcast.7, ...), custom_call_target="tpu_custom_call" | custom-call | tf_op jit(solution)/shard_map/moe/pallas_call | solution.py:485
  77.0 1.7 %copy.23 = bf16[64,2048]{1,0:T(8,128)(2,1)} copy(bf16[64,2048]{1,0:T(8,128)(2,1)} %moe.1) | data formatting | bytes 524288

commit v3 on v2

--- a/solution.py
+++ b/solution.py
@@ -159,7 +159,7 @@
     return pl.pallas_call(
         attn_kernel,
         out_shape=(
-            jax.ShapeDtypeStruct((n_b, d_model), BF16),
+            pltpu.VMEM((n_b, d_model), BF16),
             jax.ShapeDtypeStruct(k_rows.shape, BF16),
             jax.ShapeDtypeStruct(v_rows.shape, BF16),
         ),
@@ -183,18 +183,19 @@
     )(seq_lens, hidden, rope_cos, rope_sin, ln_scale, ln_bias, b_qkv, w_qkv, k_rows, v_rows, w_out)
 
 
-def moe_kernel(n_tp, n_ep, part_in, hid_in, bout_in, lns_in, lnb_in, wr_in, ids_in, wg_hbm, wu_hbm, wd_hbm,
+def moe_kernel(n_tp, n_ep, part_ref, hid_in, bout_in, lns_in, lnb_in, wr_in, ids_in, wg_hbm, wu_hbm, wd_hbm,
                out_ref,
-               part_ref, hid_ref, bout_ref, lns_ref, lnb_ref, wr_ref, ids_ref, in_sem,
-               gubuf, dbuf, hall, arx, x1buf, dmat, cmat, xbuf, abuf, ybuf, pbuf, rbuf, obuf,
-               gsem, usem, dsem, a_send, a_recv, h_send, h_recv, r_send, r_recv, o_send, o_recv):
+               hid_ref, bout_ref, lns_ref, lnb_ref, wr_ref, ids_ref, in_sem,
+               ring, hall, arx, x1buf, dmat, cmat, xbuf, abuf, ybuf, pbuf, rbuf, obuf,
+               gu_sem, d_sem, a_send, a_recv, h_send, h_recv, r_send, r_recv, o_send, o_recv):
     me_t = lax.axis_index("tp")
     me_e = lax.axis_index("ep")
     n_dev = n_tp * n_ep
     me = me_e * n_tp + me_t
-    n_gu, d_model, _ = gubuf.shape
-    width = wg_hbm.shape[2]
-    n_dr, d_group, _, d_cols = dbuf.shape
+    n_slot, d_rows, d_cols = ring.shape
+    d_model, width = wg_hbm.shape[1:]
+    edge = width - d_cols
+    d_group = d_rows // width
     n_local = wg_hbm.shape[0]
     n_exp = n_local * n_ep
     half = x1buf.shape[0]
@@ -206,44 +207,43 @@
     n_down = n_col * n_grp
     x_group = xbuf.shape[0] // cap
     n_xg = n_local // x_group
-    n_unroll = 2
+    n_unroll = 4
 
     def peer_of(d):
         pid = lax.rem(me + d, n_dev)
         return pid, {"tp": lax.rem(pid, n_tp), "ep": lax.div(pid, n_tp)}
 
-    def g_copy(i):
-        slot = lax.rem(i, n_gu)
-        return pltpu.make_async_copy(wg_hbm.at[i], gubuf.at[slot, :, pl.ds(0, width)], gsem.at[slot])
-
-    def u_copy(i):
-        slot = lax.rem(i, n_gu)
-        return pltpu.make_async_copy(wu_hbm.at[i], gubuf.at[slot, :, pl.ds(width, width)], usem.at[slot])
+    def gu_copies(i):
+        slot = lax.rem(i, n_slot)
+        top, mid, low = (pl.ds(n * d_model, d_model) for n in range(3))
+        left, right = pl.ds(0, edge), pl.ds(edge, edge)
+        pieces = (
+            (wg_hbm.at[i, :, pl.ds(0, d_cols)], ring.at[slot, top]),
+            (wg_hbm.at[i, :, pl.ds(d_cols, edge)], ring.at[slot, mid, left]),
+            (wu_hbm.at[i, :, pl.ds(0, edge)], ring.at[slot, mid, right]),
+            (wu_hbm.at[i, :, pl.ds(edge, d_cols)], ring.at[slot, low]))
+        return [pltpu.make_async_copy(src, dst, gu_sem.at[slot, n]) for n, (src, dst) in enumerate(pieces)]
 
     def d_copy(q):
-        slot = lax.rem(q, n_dr)
+        slot = lax.rem(n_local + q, n_slot)
         grp = lax.rem(q, n_grp)
         col = lax.div(q, n_grp)
-        src = wd_hbm.at[pl.ds(grp * d_group, d_group), :, pl.ds(pl.multiple_of(col * d_cols, d_cols), d_cols)]
-        return pltpu.make_async_copy(src, dbuf.at[slot], dsem.at[slot])
-
-    def first_gu(i, _):
-        g_copy(i).start()
-        u_copy(i).start()
-        return 0
-
-    def first_d(q, _):
-        d_copy(q).start()
+        src = wd_hbm.at[pl.ds(pl.multiple_of(grp * d_rows, d_rows), d_rows),
+                        pl.ds(pl.multiple_of(col * d_cols, d_cols), d_cols)]
+        return pltpu.make_async_copy(src, ring.at[slot], d_sem.at[slot])
+
+    def start_gu(i, _=0):
+        for copy in gu_copies(i):
+            copy.start()
         return 0
 
     barrier = pltpu.get_barrier_semaphore()
     for d in range(1, n_dev):
         _, dev = peer_of(d)
         pl.semaphore_signal(barrier, inc=1, device_id=dev, device_id_type=MESH)
-    small = load_all((part_in, hid_in, bout_in, lns_in, lnb_in, wr_in, ids_in),
-                     (part_ref, hid_ref, bout_ref, lns_ref, lnb_ref, wr_ref, ids_ref), in_sem)
-    lax.fori_loop(0, n_gu, first_gu, 0)
-    lax.fori_loop(0, n_dr, first_d, 0)
+    small = load_all((hid_in, bout_in, lns_in, lnb_in, wr_in, ids_in),
+                     (hid_ref, bout_ref, lns_ref, lnb_ref, wr_ref, ids_ref), in_sem)
+    lax.fori_loop(0, n_slot, start_gu, 0)
     for copy in small:
         copy.wait()
     pl.semaphore_wait(barrier, n_dev - 1)
@@ -341,23 +341,30 @@
         def some_experts(k, _):
             first = g * x_group + k * n_unroll
             for u in range(n_unroll):
-                g_copy(first + u).wait()
-                u_copy(first + u).wait()
-            both = []
+                for copy in gu_copies(first + u):
+                    copy.wait()
+            parts = []
             for u in range(n_unroll):
+                slot = lax.rem(first + u, n_slot)
                 x = xbuf[pl.ds(pl.multiple_of((k * n_unroll + u) * cap, cap), cap), :]
-                both.append(jnp.dot(x, gubuf[lax.rem(first + u, n_gu)], preferred_element_type=F32))
+                parts.append([jnp.dot(x, ring[slot, n * d_model:(n + 1) * d_model, :], preferred_element_type=F32)
+                              for n in range(3)])
             for u in range(n_unroll):
-                gate_pre, up_pre = both[u][:, :width], both[u][:, width:]
+                top, mid, low = parts[u]
+                gate_pre = jnp.concatenate([top, mid[:, :edge]], axis=1)
+                up_pre = jnp.concatenate([mid[:, edge:], low], axis=1)
                 act = (gate_pre * jax.nn.sigmoid(gate_pre) * up_pre).astype(BF16)
                 abuf[pl.ds(pl.multiple_of((first + u) * cap, cap), cap), :] = act
             for u in range(n_unroll):
-                i = first + u
-
-                @pl.when(i + n_gu < n_local)
+                item = first + u + n_slot
+
+                @pl.when(item < n_local)
                 def _():
-                    g_copy(i + n_gu).start()
-                    u_copy(i + n_gu).start()
+                    start_gu(item)
+
+                @pl.when((item >= n_local) & (item < n_local + n_down))
+                def _():
+                    d_copy(item - n_local).start()
 
             return 0
 
@@ -409,30 +416,32 @@
     def one_col(j, _):
         def one_part(g, _):
             q = j * n_grp + g
-            slot = lax.rem(q, n_dr)
-            d_copy(q).wait()
-            main = width // 256 * 256
-            rest = width - main
-            pad = jnp.zeros((cap, rest), BF16)
+            slot = lax.rem(n_local + q, n_slot)
+            main = width - edge
+            pad = jnp.zeros((cap, edge), BF16)
             for k in range(0, d_group, 2):
                 rows = [pl.ds(pl.multiple_of((g * d_group + k + u) * cap, cap), cap) for u in range(2)]
                 acts = [abuf[rows[u], :] for u in range(2)]
                 ends = jnp.concatenate([
                     jnp.concatenate([acts[0][:, main:], pad], axis=1),
                     jnp.concatenate([pad, acts[1][:, main:]], axis=1)], axis=0)
-                end_w = jnp.concatenate([dbuf[slot, k, main:, :], dbuf[slot, k + 1, main:, :]], axis=0)
+                end_w = jnp.concatenate([ring[slot, (k + u) * width + main:(k + u + 1) * width, :] for u in range(2)], axis=0)
                 tail = jnp.dot(ends, end_w, preferred_element_type=F32)
                 for u in range(2):
-                    y = jnp.dot(acts[u][:, :main], dbuf[slot, k + u, :main, :], preferred_element_type=F32)
+                    top = (k + u) * width
+                    y = jnp.dot(acts[u][:, :main], ring[slot, top:top + main, :], preferred_element_type=F32)
                     ybuf[rows[u], :] = (y + tail[u * cap:(u + 1) * cap]).astype(BF16)
 
-            @pl.when(q + n_dr < n_down)
+            @pl.when(q + n_slot < n_down)
             def _():
-                d_copy(q + n_dr).start()
+                d_copy(q + n_slot).start()
 
             return 0
 
-        lax.fori_loop(0, n_grp, one_part, 0)
+        for g in range(n_grp):
+            d_copy(j * n_grp + g).wait()
+        for g in range(n_grp):
+            one_part(g, 0)
         for u in range(2):
             part_rows = slice(u * n_rows // 2, (u + 1) * n_rows // 2)
             pbuf[j, part_rows, :] = jnp.dot(cmat[part_rows, :], ybuf[...], preferred_element_type=F32).astype(BF16)
@@ -476,7 +485,7 @@
     n_dev = n_tp * n_ep
     half = n_b // n_tp
     cap = 32
-    n_gu, n_dr, d_group, d_cols = 12, 4, 16, 256
+    n_slot, d_cols = 16, 256
     n_sub = 2
     n_col = d_model // d_cols
     vmem = pl.BlockSpec(memory_space=pltpu.VMEM)
@@ -484,13 +493,12 @@
     dma = pltpu.SemaphoreType.DMA
     return pl.pallas_call(
         functools.partial(moe_kernel, n_tp, n_ep),
-        out_shape=jax.ShapeDtypeStruct((n_b, d_model), BF16),
-        in_specs=[hbm] * 10,
+        out_shape=pltpu.VMEM((n_b, d_model), BF16),
+        in_specs=[vmem] + [hbm] * 9,
         out_specs=vmem,
-        scratch_shapes=[pltpu.VMEM(x.shape, x.dtype) for x in (part, hidden, b_out, ln_scale, ln_bias, w_router, ids_t)] + [
-            dma((7,)),
-            pltpu.VMEM((n_gu, d_model, 2 * width), BF16),
-            pltpu.VMEM((n_dr, d_group, width, d_cols), BF16),
+        scratch_shapes=[pltpu.VMEM(x.shape, x.dtype) for x in (hidden, b_out, ln_scale, ln_bias, w_router, ids_t)] + [
+            dma((6,)),
+            pltpu.VMEM((n_slot, 3 * d_model, d_cols), BF16),
             pltpu.VMEM((n_rows, d_model + n_exp), BF16),
             pltpu.VMEM((half, d_model), BF16),
             pltpu.VMEM((half, d_model), BF16),
@@ -502,11 +510,11 @@
             pltpu.VMEM((n_col, n_rows, d_cols), BF16),
             pltpu.VMEM((n_col, n_dev, half, d_cols), BF16),
             pltpu.VMEM((n_col, n_tp, half, d_cols), BF16),
-            dma((n_gu,)), dma((n_gu,)), dma((n_dr,)), dma((n_sub,)), dma((n_sub,)), dma((7, n_sub)), dma((n_dev, n_sub)),
+            dma((n_slot, 4)), dma((n_slot,)), dma((n_sub,)), dma((n_sub,)), dma((7, n_sub)), dma((n_dev, n_sub)),
             dma((n_col, n_dev)), dma((n_col, n_dev)), dma((n_col,)), dma((n_col,)),
         ],
         compiler_params=pltpu.CompilerParams(
-            collective_id=0, has_side_effects=True, vmem_limit_bytes=67043328),
+            collective_id=0, has_side_effects=True, vmem_limit_bytes=65700000),
         name="moe",
     )(part, hidden, b_out, ln_scale, ln_bias, w_router, ids_t, w_gate, w_up, w_down)
 
@@ -525,8 +533,10 @@
         v_rows = v_cache.reshape(n_b, s_max * n_groups, head)
         part, k_out, v_out = attention_call(
             hidden, seq_lens, rope_cos, rope_sin, ln1_scale, ln1_bias, w_qkv, b_qkv, w_out, k_rows, v_rows)
+        part = pltpu.with_memory_space_constraint(part, pltpu.VMEM)
         hidden_out = moe_call(
-            n_tp, n_ep, part, hidden, b_out, ln2_scale, ln2_bias, w_router, expert_ids.T, w_gate, w_up, w_down)
+            n_tp, n_ep, part, hidden, b_out, ln2_scale, ln2_bias, w_router, expert_ids.T, w_gate, w_up,
+            w_down.reshape(-1, w_down.shape[2]))
         return hidden_out, k_out.reshape(k_cache.shape), v_out.reshape(v_cache.shape)
 
     in_specs = (token_rows, token_vec, token_rows, token_rows, P(), P(), P(None, 'tp'), P('tp'), P('tp', None), P(), cache_spec, cache_spec, P(), P(), P(), token_rows, expert_in, expert_in, expert_down)

time: 78.8 us -> 75.2 us (0.954)
  Pallas kernels: 76.3 us -> 73.8 us
  local copies, waits for them, and re-layouts: 1.67 us -> 0.71 us
    pallas_call x2, Pallas kernels: 76.3 us -> 73.8 us  [the longest x1 60 us: moe_call(): pl.pallas_call(functools.partial(moe_kernel, n_tp, n_ep), out_shape=pltpu...]
    unnamed x1, local copies, waits for them, and re-layouts: 1.67 us -> 0.71 us
where the time goes in v3:
time: 75.2 us; the launch traced here: 75.1 us
  Pallas kernels  73.8 us (98%)
    pallas_call x1, Pallas kernels, moe_call(): pl.pallas_call(functools.partial(moe_kernel, n_tp, n_ep), out_shape=pltpu...  60 us
    pallas_call x1, Pallas kernels, attention_call(): pl.pallas_call(attn_kernel, out_shape=(pltpu.VMEM((n_b, d_model), BF16),...  13.8 us

profile of v3, /device:TPU:0, one launch (start us, length us, event | category | flops | bytes accessed | tf_op | source)
XLA Modules:
  0.0 75.1 jit_solution(18055602281895818239)
XLA Ops:
  0.6 13.8 %attn.1 = (bf16[64,2048]{1,0:T(8,128)(2,1)S(1)}, bf16[64,256,128]{2,1,0:T(8,128)(2,1)}, bf16[64,256,128]{2,1,0:T(8,128)(2,1)}) custom-call(s32[64]{0:T(128)} %seq_ref.1, bf16[64,2048]{1,0:T(8,128)(2,1)} %hid_in.1, f32[64,64]{1,0:T(8,128)} %cos_ref.1, f32[64,64]{1,0:T(8,128)} %sin_ref.1, bf16[2048]{0:T(1024)(128)(2,1)} %lns_ref.1, bf16[2048]{0:T(1024)(128)(2,1)} %lnb_ref.1, ...), custom_call_target="tpu_custom_call" | custom-call | tf_op jit(solution)/shard_map/attn/pallas_call | solution.py:159
  14.4 60.0 %moe.1 = bf16[64,2048]{1,0:T(8,128)(2,1)S(1)} custom-call(bf16[64,2048]{1,0:T(8,128)(2,1)S(1)} %get-tuple-element.6.part_ref, bf16[64,2048]{1,0:T(8,128)(2,1)} %hid_in.1, bf16[2048]{0:T(1024)(128)(2,1)} %bout_in.1, bf16[2048]{0:T(1024)(128)(2,1)} %lns_in.1, bf16[2048]{0:T(1024)(128)(2,1)} %lnb_in.1, bf16[2048,128]{1,0:T(8,128)(2,1)} %wr_in.1, ...), custom_call_target="tpu_custom_call" | custom-call | tf_op jit(solution)/shard_map/moe/pallas_call | solution.py:494
  74.4 0.7 copy.23
